TPU v7x, 32 devices: a whole 2x2x4 slice. The times are simulated.
32 devices in a mesh: cuts: 4 (over y, x), space: 8 (over z, core).
Axes of the slice: x: 2, y: 2, z: 4, core: 2. Of those that a mesh axis runs over, the one named last changes fastest.
Arguments:
- starts: float32 [4, 3, 32, 64, 128], P('cuts', None, 'space'), may hold values from -3 to 3
Outputs:
- new_starts: float32 [4, 3, 32, 64, 128], P('cuts', None, 'space')
All inputs are finite; a program needn't handle non-finite values.
Results may differ from a plain program's by a relative error of at most 0.0001.
Values sent between devices are 32-bit elements; how exact they have to be, the bound alone decides.
A program may use at most 64 MiB of HBM per device.

v0:
```python
import jax
import jax.numpy as jnp
from jax import lax
from jax.sharding import PartitionSpec as P

FSTEPS = 16
CSTEPS = 2


fine_rate = 0.08
fine_advect = 0.04
coarse_rate = 0.16
coarse_advect = 0.16


def padded_2(cells, sides, width):
    for axis, dim in sides:
        count = lax.axis_size(axis)
        ends = count - 1
        head = lax.slice_in_dim(cells, 0, width, axis=dim)
        tail = lax.slice_in_dim(cells, cells.shape[dim] - width, cells.shape[dim], axis=dim)
        cells = jnp.concatenate(
            [
                lax.ppermute(tail, axis, [(i, (i + 1) % count) for i in range(ends)]),
                cells,
                lax.ppermute(head, axis, [((i + 1) % count, i) for i in range(ends)]),
            ],
            axis=dim,
        )
    return cells


def passed_along(shard, axis, by):
    length = lax.axis_size(axis)
    pairs = [(i, i + by) for i in range(length) if 0 <= i + by < length]
    return lax.ppermute(shard, axis, pairs)


def advance(extended, rate, advect):
    padded = jnp.pad(extended, ((0, 0), (0, 0), (1, 1), (1, 1)))
    centre = padded[:, 1:-1, 1:-1, 1:-1]
    x_plus = padded[:, 2:, 1:-1, 1:-1]
    x_minus = padded[:, :-2, 1:-1, 1:-1]
    y_plus = padded[:, 1:-1, 2:, 1:-1]
    y_minus = padded[:, 1:-1, :-2, 1:-1]
    z_plus = padded[:, 1:-1, 1:-1, 2:]
    z_minus = padded[:, 1:-1, 1:-1, :-2]
    laplace = x_plus + x_minus + (y_plus + y_minus) + (z_plus + z_minus) - 6.0 * centre
    convect = (
        centre[0:1] * (x_plus - x_minus)
        + centre[1:2] * (y_plus - y_minus)
        + centre[2:3] * (z_plus - z_minus)
    )
    return centre + rate * laplace - advect * convect


def restrict(field):
    blocks = field.reshape(
        field.shape[0], field.shape[1] // 2, 2, field.shape[2] // 2, 2, field.shape[3] // 2, 2
    )
    return jnp.sum(blocks, axis=(2, 4, 6)) * 0.125


def prolong(field):
    return jnp.repeat(jnp.repeat(jnp.repeat(field, 2, axis=1), 2, axis=2), 2, axis=3)


def double_fine(index, field):
    width = field.shape[1]
    extended = padded_2(field, (("space", 1),), 2)
    first = advance(extended, fine_rate, fine_advect)
    global_rows = lax.axis_index("space") * width - 1 + jnp.arange(width + 2, dtype=jnp.int32)
    inside = (global_rows >= 0) & (global_rows < width * lax.axis_size("space"))
    first = jnp.where(inside[None, :, None, None], first, 0.0)
    return advance(first, fine_rate, fine_advect)


def fine_run(field):
    return lax.fori_loop(0, FSTEPS // 2, double_fine, field)


def coarse_single(index, field):
    extended = padded_2(field, (("space", 1),), 1)
    return advance(extended, coarse_rate, coarse_advect)


def coarse_run(field):
    return lax.fori_loop(0, CSTEPS, coarse_single, field)


def shards(starts):
    initial = starts[0]
    ends = fine_run(initial)
    coarse_start = restrict(initial)
    old_coarse = coarse_run(coarse_start)
    change = ends - prolong(old_coarse)
    previous = passed_along(change, "cuts", 1)
    previous_coarse = restrict(previous)
    position = lax.axis_index("cuts")
    groups = lax.axis_size("cuts")

    def relay_turn(index, carry):
        current, stored = carry
        incoming = passed_along(current, "cuts", 1)
        advanced = coarse_run(incoming)
        active = position == index + 1
        current = jnp.where(active, advanced + previous_coarse, current)
        stored = jnp.where(active, advanced, stored)
        return (current, stored)

    unused, stored = lax.fori_loop(
        0, groups - 1, relay_turn, (coarse_start, jnp.zeros_like(coarse_start))
    )
    corrected = jnp.where(position == 0, initial, prolong(stored) + previous)
    return corrected[None]


def solution(mesh):
    placed = (P("cuts", None, "space", None, None),)
    return jax.shard_map(
        shards,
        mesh=mesh,
        in_specs=placed,
        out_specs=P("cuts", None, "space", None, None),
        check_vma=False,
    )
```

profile of v0, /device:TPU:15, one launch (start us, length us, event | category | flops | bytes accessed | tf_op | source)
XLA Modules:
  0.0 251.7 jit_solution(10871689313306393494)
XLA Ops:
  0.0 27.3 %reshape_squeeze.3 = f32[3,2,2,32,2,64,2]{6,5,4,3,2,1,0:T(8,128)} reshape(f32[1,3,4,64,128]{4,3,2,1,0:T(8,128)} %param.9) | data formatting | bytes 786432 | tf_op jit(solution)/shard_map/reshape;squeeze | solution.py:58
  27.3 9.5 %reduce_sum.18 = f32[3,2,32,64]{3,2,1,0:T(8,128)S(1)} reduce(f32[3,2,2,32,2,64,2]{6,5,4,3,2,1,0:T(8,128)} %reshape_squeeze.3, f32[]{:T(128)} %constant.77.clone.1), dimensions={2,4,6}, to_apply=%region_0.1 | reduce | flops 86016 | bytes 442372 | tf_op jit(solution)/shard_map/reduce_sum | solution.py:61
  36.8 14.9 %while.60 = (s32[]{:T(128)}, f32[3,2,32,64]{3,2,1,0:T(8,128)S(1)}, s32[]{:T(128)}) while((s32[]{:T(128)}, f32[3,2,32,64]{3,2,1,0:T(8,128)S(1)}, s32[]{:T(128)}) %tuple.123), condition=%wide.region_4.5_spmd, body=%wide.region_3.4_spmd.sunk | while | flops 661970 | bytes 1090877 | solution.py:88
  36.8 2.6 %collective-permute-start.2 = (f32[3,1,32,64]{3,2,1,0:T(8,128)S(1)}, f32[3,1,32,64]{3,2,1,0:T(8,128)S(1)}, u32[]{:S(2)}, u32[]{:S(2)}) collective-permute-start(f32[3,1,32,64]{3,2,1,0:T(8,128)S(1)} %get-tuple-element.324), channel_id=1, source_target_pairs={{1,0},{2,1},{3,2},{4,3},{5,4},{6,5},{7,6},{9,8},{10,9},{11,10},{12... | collective-permute-start | bytes 73736 | tf_op jit(solution)/shard_map/while/body/eval_jaxpr/ppermute | solution.py:26
  39.4 3.1 %collective-permute-start.3 = (f32[3,1,32,64]{3,2,1,0:T(8,128)S(1)}, f32[3,1,32,64]{3,2,1,0:T(8,128)S(1)}, u32[]{:S(2)}, u32[]{:S(2)}) collective-permute-start(f32[3,1,32,64]{3,2,1,0:T(8,128)S(1)} %get-tuple-element.325), channel_id=1, source_target_pairs={{0,1},{1,2},{2,3},{3,4},{4,5},{5,6},{6,7},{8,9},{9,10},{10,11},{11... | collective-permute-start | bytes 73736 | tf_op jit(solution)/shard_map/while/body/eval_jaxpr/ppermute | solution.py:24
  44.0 3.1 %collective-permute-start.2 = (f32[3,1,32,64]{3,2,1,0:T(8,128)S(1)}, f32[3,1,32,64]{3,2,1,0:T(8,128)S(1)}, u32[]{:S(2)}, u32[]{:S(2)}) collective-permute-start(f32[3,1,32,64]{3,2,1,0:T(8,128)S(1)} %get-tuple-element.324), channel_id=1, source_target_pairs={{1,0},{2,1},{3,2},{4,3},{5,4},{6,5},{7,6},{9,8},{10,9},{11,10},{12... | collective-permute-start | bytes 73736 | tf_op jit(solution)/shard_map/while/body/eval_jaxpr/ppermute | solution.py:26
  47.1 3.1 %collective-permute-start.3 = (f32[3,1,32,64]{3,2,1,0:T(8,128)S(1)}, f32[3,1,32,64]{3,2,1,0:T(8,128)S(1)}, u32[]{:S(2)}, u32[]{:S(2)}) collective-permute-start(f32[3,1,32,64]{3,2,1,0:T(8,128)S(1)} %get-tuple-element.325), channel_id=1, source_target_pairs={{0,1},{1,2},{2,3},{3,4},{4,5},{5,6},{6,7},{8,9},{9,10},{10,11},{11... | collective-permute-start | bytes 73736 | tf_op jit(solution)/shard_map/while/body/eval_jaxpr/ppermute | solution.py:24
  52.6 82.7 %while.59 = (s32[]{:T(128)}, f32[3,4,64,128]{3,2,1,0:T(8,128)S(1)}, s32[]{:T(128)}, u32[]{:T(128)}, s32[]{:T(128)}, /*index=5*/s32[]{:T(128)}) while((s32[]{:T(128)}, f32[3,4,64,128]{3,2,1,0:T(8,128)S(1)}, s32[]{:T(128)}, u32[]{:T(128)}, s32[]{:T(128)}, /*index=5*/s32[]{:T(128)}) %tuple.120), condition=%wide.region_2.3_spmd, body=%wide.region_1.2_spmd.sunk | while | flops 4816926 | bytes 13370059 | solution.py:79
  52.6 4.2 %collective-permute-start = (f32[3,2,64,128]{3,2,1,0:T(8,128)S(1)}, f32[3,2,64,128]{3,2,1,0:T(8,128)S(1)}, u32[]{:S(2)}, u32[]{:S(2)}) collective-permute-start(f32[3,2,64,128]{3,2,1,0:T(8,128)S(1)} %get-tuple-element.307), channel_id=1, source_target_pairs={{0,1},{1,2},{2,3},{3,4},{4,5},{5,6},{6,7},{8,9},{9,10},{10,11},{11... | collective-permute-start | bytes 589832 | tf_op jit(solution)/shard_map/while/body/eval_jaxpr/ppermute | solution.py:24
  56.9 1.9 collective-permute-start.1
  59.7 4.2 %collective-permute-done.1 = f32[3,2,64,128]{3,2,1,0:T(8,128)S(1)} collective-permute-done((f32[3,2,64,128]{3,2,1,0:T(8,128)S(1)}, f32[3,2,64,128]{3,2,1,0:T(8,128)S(1)}, u32[]{:S(2)}, u32[]{:S(2)}) %collective-permute-start.1) | collective-permute-done | bytes 196640 | tf_op jit(solution)/shard_map/while/body/eval_jaxpr/ppermute | solution.py:26
  65.0 1.9 collective-permute-start
  66.9 2.4 collective-permute-start.1
  69.7 4.2 %collective-permute-done.1 = f32[3,2,64,128]{3,2,1,0:T(8,128)S(1)} collective-permute-done((f32[3,2,64,128]{3,2,1,0:T(8,128)S(1)}, f32[3,2,64,128]{3,2,1,0:T(8,128)S(1)}, u32[]{:S(2)}, u32[]{:S(2)}) %collective-permute-start.1) | collective-permute-done | bytes 196640 | tf_op jit(solution)/shard_map/while/body/eval_jaxpr/ppermute | solution.py:26
  77.0 2.4 collective-permute-start.1
  79.7 4.2 %collective-permute-done.1 = f32[3,2,64,128]{3,2,1,0:T(8,128)S(1)} collective-permute-done((f32[3,2,64,128]{3,2,1,0:T(8,128)S(1)}, f32[3,2,64,128]{3,2,1,0:T(8,128)S(1)}, u32[]{:S(2)}, u32[]{:S(2)}) %collective-permute-start.1) | collective-permute-done | bytes 196640 | tf_op jit(solution)/shard_map/while/body/eval_jaxpr/ppermute | solution.py:26
  87.0 2.4 collective-permute-start.1
  89.8 4.2 %collective-permute-done.1 = f32[3,2,64,128]{3,2,1,0:T(8,128)S(1)} collective-permute-done((f32[3,2,64,128]{3,2,1,0:T(8,128)S(1)}, f32[3,2,64,128]{3,2,1,0:T(8,128)S(1)}, u32[]{:S(2)}, u32[]{:S(2)}) %collective-permute-start.1) | collective-permute-done | bytes 196640 | tf_op jit(solution)/shard_map/while/body/eval_jaxpr/ppermute | solution.py:26
  97.1 2.4 collective-permute-start.1
  99.8 4.2 %collective-permute-done.1 = f32[3,2,64,128]{3,2,1,0:T(8,128)S(1)} collective-permute-done((f32[3,2,64,128]{3,2,1,0:T(8,128)S(1)}, f32[3,2,64,128]{3,2,1,0:T(8,128)S(1)}, u32[]{:S(2)}, u32[]{:S(2)}) %collective-permute-start.1) | collective-permute-done | bytes 196640 | tf_op jit(solution)/shard_map/while/body/eval_jaxpr/ppermute | solution.py:26
  107.1 2.4 collective-permute-start.1
  109.9 4.2 %collective-permute-done.1 = f32[3,2,64,128]{3,2,1,0:T(8,128)S(1)} collective-permute-done((f32[3,2,64,128]{3,2,1,0:T(8,128)S(1)}, f32[3,2,64,128]{3,2,1,0:T(8,128)S(1)}, u32[]{:S(2)}, u32[]{:S(2)}) %collective-permute-start.1) | collective-permute-done | bytes 196640 | tf_op jit(solution)/shard_map/while/body/eval_jaxpr/ppermute | solution.py:26
  117.1 2.4 collective-permute-start.1
  119.9 4.2 %collective-permute-done.1 = f32[3,2,64,128]{3,2,1,0:T(8,128)S(1)} collective-permute-done((f32[3,2,64,128]{3,2,1,0:T(8,128)S(1)}, f32[3,2,64,128]{3,2,1,0:T(8,128)S(1)}, u32[]{:S(2)}, u32[]{:S(2)}) %collective-permute-start.1) | collective-permute-done | bytes 196640 | tf_op jit(solution)/shard_map/while/body/eval_jaxpr/ppermute | solution.py:26
  127.2 2.4 collective-permute-start.1
  130.0 4.2 %collective-permute-done.1 = f32[3,2,64,128]{3,2,1,0:T(8,128)S(1)} collective-permute-done((f32[3,2,64,128]{3,2,1,0:T(8,128)S(1)}, f32[3,2,64,128]{3,2,1,0:T(8,128)S(1)}, u32[]{:S(2)}, u32[]{:S(2)}) %collective-permute-start.1) | collective-permute-done | bytes 196640 | tf_op jit(solution)/shard_map/while/body/eval_jaxpr/ppermute | solution.py:26
  136.9 10.3 %collective-permute-done.7 = f32[3,4,64,128]{3,2,1,0:T(8,128)S(1)} collective-permute-done((f32[3,4,64,128]{3,2,1,0:T(8,128)S(1)}, f32[3,4,64,128]{3,2,1,0:T(8,128)S(1)}, u32[]{:S(2)}, u32[]{:S(2)}) %collective-permute-start.7) | collective-permute-done | bytes 393248 | tf_op jit(solution)/shard_map/ppermute | solution.py:36
  147.2 26.5 %reshape.31 = f32[3,2,2,32,2,64,2]{6,5,4,3,2,1,0:T(8,128)} reshape(f32[3,4,64,128]{3,2,1,0:T(8,128)S(1)} %collective-permute-done.7) | data formatting | bytes 786432 | tf_op jit(solution)/shard_map/reshape | solution.py:58
  173.7 9.4 %reduce_sum.19 = f32[3,2,32,64]{3,2,1,0:T(8,128)S(1)} reduce(f32[3,2,2,32,2,64,2]{6,5,4,3,2,1,0:T(8,128)} %reshape.31, f32[]{:T(128)} %constant.77.clone.1), dimensions={2,4,6}, to_apply=%region_5.6 | reduce | flops 86016 | bytes 442372 | tf_op jit(solution)/shard_map/reduce_sum | solution.py:61
  183.1 66.5 %while.62 = (s32[]{:T(128)}, f32[3,2,32,64]{3,2,1,0:T(8,128)S(1)}, f32[3,2,32,64]{3,2,1,0:T(8,128)S(1)}, s32[]{:T(128)}, f32[3,2,32,64]{3,2,1,0:T(8,128)S(1)}, /*index=5*/s32[]{:T(128)}, s32[]{:T(128)}, s32[]{:T(128)}) while((s32[]{:T(128)}, f32[3,2,32,64]{3,2,1,0:T(8,128)S(1)}, f32[3,2,32,64]{3,2,1,0:T(8,128)S(1)}, s32[]{:T(128)}, ...), condition=%wide.region_9.10_spmd.clone, body=%wide.region_6.9_spmd.clone.sunk | while | flops 711126 | bytes 1582574 | solution.py:111
  184.4 5.1 %collective-permute-done.6 = f32[3,2,32,64]{3,2,1,0:T(8,128)S(1)} collective-permute-done((f32[3,2,32,64]{3,2,1,0:T(8,128)S(1)}, f32[3,2,32,64]{3,2,1,0:T(8,128)S(1)}, u32[]{:S(2)}, u32[]{:S(2)}) %collective-permute-start.6) | collective-permute-done | bytes 49184 | tf_op jit(solution)/shard_map/while/body/eval_jaxpr/ppermute | solution.py:36
  189.6 14.9 %while.63 = (s32[]{:T(128)}, f32[3,2,32,64]{3,2,1,0:T(8,128)S(1)}, s32[]{:T(128)}) while((s32[]{:T(128)}, f32[3,2,32,64]{3,2,1,0:T(8,128)S(1)}, s32[]{:T(128)}) %tuple.117), condition=%wide.region_8.8_spmd, body=%wide.region_7.7_spmd.sunk | while | flops 661970 | bytes 1090877 | solution.py:88
  189.6 2.6 %collective-permute-start.4 = (f32[3,1,32,64]{3,2,1,0:T(8,128)S(1)}, f32[3,1,32,64]{3,2,1,0:T(8,128)S(1)}, u32[]{:S(2)}, u32[]{:S(2)}) collective-permute-start(f32[3,1,32,64]{3,2,1,0:T(8,128)S(1)} %get-tuple-element.340), channel_id=1, source_target_pairs={{1,0},{2,1},{3,2},{4,3},{5,4},{6,5},{7,6},{9,8},{10,9},{11,10},{12... | collective-permute-start | bytes 73736 | tf_op jit(solution)/shard_map/while/body/eval_jaxpr/while/body/eval_jaxpr/ppermute | solution.py:26
  192.2 3.1 %collective-permute-start.5 = (f32[3,1,32,64]{3,2,1,0:T(8,128)S(1)}, f32[3,1,32,64]{3,2,1,0:T(8,128)S(1)}, u32[]{:S(2)}, u32[]{:S(2)}) collective-permute-start(f32[3,1,32,64]{3,2,1,0:T(8,128)S(1)} %get-tuple-element.341), channel_id=1, source_target_pairs={{0,1},{1,2},{2,3},{3,4},{4,5},{5,6},{6,7},{8,9},{9,10},{10,11},{11... | collective-permute-start | bytes 73736 | tf_op jit(solution)/shard_map/while/body/eval_jaxpr/while/body/eval_jaxpr/ppermute | solution.py:24
  196.8 3.1 %collective-permute-start.4 = (f32[3,1,32,64]{3,2,1,0:T(8,128)S(1)}, f32[3,1,32,64]{3,2,1,0:T(8,128)S(1)}, u32[]{:S(2)}, u32[]{:S(2)}) collective-permute-start(f32[3,1,32,64]{3,2,1,0:T(8,128)S(1)} %get-tuple-element.340), channel_id=1, source_target_pairs={{1,0},{2,1},{3,2},{4,3},{5,4},{6,5},{7,6},{9,8},{10,9},{11,10},{12... | collective-permute-start | bytes 73736 | tf_op jit(solution)/shard_map/while/body/eval_jaxpr/while/body/eval_jaxpr/ppermute | solution.py:26
  199.9 3.1 %collective-permute-start.5 = (f32[3,1,32,64]{3,2,1,0:T(8,128)S(1)}, f32[3,1,32,64]{3,2,1,0:T(8,128)S(1)}, u32[]{:S(2)}, u32[]{:S(2)}) collective-permute-start(f32[3,1,32,64]{3,2,1,0:T(8,128)S(1)} %get-tuple-element.341), channel_id=1, source_target_pairs={{0,1},{1,2},{2,3},{3,4},{4,5},{5,6},{6,7},{8,9},{9,10},{10,11},{11... | collective-permute-start | bytes 73736 | tf_op jit(solution)/shard_map/while/body/eval_jaxpr/while/body/eval_jaxpr/ppermute | solution.py:24
  205.8 4.7 %collective-permute-done.6 = f32[3,2,32,64]{3,2,1,0:T(8,128)S(1)} collective-permute-done((f32[3,2,32,64]{3,2,1,0:T(8,128)S(1)}, f32[3,2,32,64]{3,2,1,0:T(8,128)S(1)}, u32[]{:S(2)}, u32[]{:S(2)}) %collective-permute-start.6) | collective-permute-done | bytes 49184 | tf_op jit(solution)/shard_map/while/body/eval_jaxpr/ppermute | solution.py:36
  210.5 16.2 %while.63 = (s32[]{:T(128)}, f32[3,2,32,64]{3,2,1,0:T(8,128)S(1)}, s32[]{:T(128)}) while((s32[]{:T(128)}, f32[3,2,32,64]{3,2,1,0:T(8,128)S(1)}, s32[]{:T(128)}) %tuple.117), condition=%wide.region_8.8_spmd, body=%wide.region_7.7_spmd.sunk | while | flops 661970 | bytes 1090877 | solution.py:88
  210.5 3.9 %collective-permute-start.4 = (f32[3,1,32,64]{3,2,1,0:T(8,128)S(1)}, f32[3,1,32,64]{3,2,1,0:T(8,128)S(1)}, u32[]{:S(2)}, u32[]{:S(2)}) collective-permute-start(f32[3,1,32,64]{3,2,1,0:T(8,128)S(1)} %get-tuple-element.340), channel_id=1, source_target_pairs={{1,0},{2,1},{3,2},{4,3},{5,4},{6,5},{7,6},{9,8},{10,9},{11,10},{12... | collective-permute-start | bytes 73736 | tf_op jit(solution)/shard_map/while/body/eval_jaxpr/while/body/eval_jaxpr/ppermute | solution.py:26
  214.4 3.1 %collective-permute-start.5 = (f32[3,1,32,64]{3,2,1,0:T(8,128)S(1)}, f32[3,1,32,64]{3,2,1,0:T(8,128)S(1)}, u32[]{:S(2)}, u32[]{:S(2)}) collective-permute-start(f32[3,1,32,64]{3,2,1,0:T(8,128)S(1)} %get-tuple-element.341), channel_id=1, source_target_pairs={{0,1},{1,2},{2,3},{3,4},{4,5},{5,6},{6,7},{8,9},{9,10},{10,11},{11... | collective-permute-start | bytes 73736 | tf_op jit(solution)/shard_map/while/body/eval_jaxpr/while/body/eval_jaxpr/ppermute | solution.py:24
  219.1 3.1 %collective-permute-start.4 = (f32[3,1,32,64]{3,2,1,0:T(8,128)S(1)}, f32[3,1,32,64]{3,2,1,0:T(8,128)S(1)}, u32[]{:S(2)}, u32[]{:S(2)}) collective-permute-start(f32[3,1,32,64]{3,2,1,0:T(8,128)S(1)} %get-tuple-element.340), channel_id=1, source_target_pairs={{1,0},{2,1},{3,2},{4,3},{5,4},{6,5},{7,6},{9,8},{10,9},{11,10},{12... | collective-permute-start | bytes 73736 | tf_op jit(solution)/shard_map/while/body/eval_jaxpr/while/body/eval_jaxpr/ppermute | solution.py:26
  222.1 3.1 %collective-permute-start.5 = (f32[3,1,32,64]{3,2,1,0:T(8,128)S(1)}, f32[3,1,32,64]{3,2,1,0:T(8,128)S(1)}, u32[]{:S(2)}, u32[]{:S(2)}) collective-permute-start(f32[3,1,32,64]{3,2,1,0:T(8,128)S(1)} %get-tuple-element.341), channel_id=1, source_target_pairs={{0,1},{1,2},{2,3},{3,4},{4,5},{5,6},{6,7},{8,9},{9,10},{10,11},{11... | collective-permute-start | bytes 73736 | tf_op jit(solution)/shard_map/while/body/eval_jaxpr/while/body/eval_jaxpr/ppermute | solution.py:24
  228.1 5.2 %collective-permute-done.6 = f32[3,2,32,64]{3,2,1,0:T(8,128)S(1)} collective-permute-done((f32[3,2,32,64]{3,2,1,0:T(8,128)S(1)}, f32[3,2,32,64]{3,2,1,0:T(8,128)S(1)}, u32[]{:S(2)}, u32[]{:S(2)}) %collective-permute-start.6) | collective-permute-done | bytes 49184 | tf_op jit(solution)/shard_map/while/body/eval_jaxpr/ppermute | solution.py:36
  233.3 16.2 %while.63 = (s32[]{:T(128)}, f32[3,2,32,64]{3,2,1,0:T(8,128)S(1)}, s32[]{:T(128)}) while((s32[]{:T(128)}, f32[3,2,32,64]{3,2,1,0:T(8,128)S(1)}, s32[]{:T(128)}) %tuple.117), condition=%wide.region_8.8_spmd, body=%wide.region_7.7_spmd.sunk | while | flops 661970 | bytes 1090877 | solution.py:88
  233.4 3.9 %collective-permute-start.4 = (f32[3,1,32,64]{3,2,1,0:T(8,128)S(1)}, f32[3,1,32,64]{3,2,1,0:T(8,128)S(1)}, u32[]{:S(2)}, u32[]{:S(2)}) collective-permute-start(f32[3,1,32,64]{3,2,1,0:T(8,128)S(1)} %get-tuple-element.340), channel_id=1, source_target_pairs={{1,0},{2,1},{3,2},{4,3},{5,4},{6,5},{7,6},{9,8},{10,9},{11,10},{12... | collective-permute-start | bytes 73736 | tf_op jit(solution)/shard_map/while/body/eval_jaxpr/while/body/eval_jaxpr/ppermute | solution.py:26
  237.3 3.1 %collective-permute-start.5 = (f32[3,1,32,64]{3,2,1,0:T(8,128)S(1)}, f32[3,1,32,64]{3,2,1,0:T(8,128)S(1)}, u32[]{:S(2)}, u32[]{:S(2)}) collective-permute-start(f32[3,1,32,64]{3,2,1,0:T(8,128)S(1)} %get-tuple-element.341), channel_id=1, source_target_pairs={{0,1},{1,2},{2,3},{3,4},{4,5},{5,6},{6,7},{8,9},{9,10},{10,11},{11... | collective-permute-start | bytes 73736 | tf_op jit(solution)/shard_map/while/body/eval_jaxpr/while/body/eval_jaxpr/ppermute | solution.py:24
  241.9 3.1 %collective-permute-start.4 = (f32[3,1,32,64]{3,2,1,0:T(8,128)S(1)}, f32[3,1,32,64]{3,2,1,0:T(8,128)S(1)}, u32[]{:S(2)}, u32[]{:S(2)}) collective-permute-start(f32[3,1,32,64]{3,2,1,0:T(8,128)S(1)} %get-tuple-element.340), channel_id=1, source_target_pairs={{1,0},{2,1},{3,2},{4,3},{5,4},{6,5},{7,6},{9,8},{10,9},{11,10},{12... | collective-permute-start | bytes 73736 | tf_op jit(solution)/shard_map/while/body/eval_jaxpr/while/body/eval_jaxpr/ppermute | solution.py:26
  245.0 3.1 %collective-permute-start.5 = (f32[3,1,32,64]{3,2,1,0:T(8,128)S(1)}, f32[3,1,32,64]{3,2,1,0:T(8,128)S(1)}, u32[]{:S(2)}, u32[]{:S(2)}) collective-permute-start(f32[3,1,32,64]{3,2,1,0:T(8,128)S(1)} %get-tuple-element.341), channel_id=1, source_target_pairs={{0,1},{1,2},{2,3},{3,4},{4,5},{5,6},{6,7},{8,9},{9,10},{10,11},{11... | collective-permute-start | bytes 73736 | tf_op jit(solution)/shard_map/while/body/eval_jaxpr/while/body/eval_jaxpr/ppermute | solution.py:24
  (170 shorter events, 43.3 us)
Async XLA Ops:
  27.3 25.3 %copy-start = (f32[1,3,4,64,128]{4,3,2,1,0:T(8,128)S(1)}, f32[1,3,4,64,128]{4,3,2,1,0:T(8,128)}, u32[]{:S(2)}) copy-start(f32[1,3,4,64,128]{4,3,2,1,0:T(8,128)} %param.9) | copy-start | bytes 1179652
  36.8 5.7 %collective-permute-start.2 = (f32[3,1,32,64]{3,2,1,0:T(8,128)S(1)}, f32[3,1,32,64]{3,2,1,0:T(8,128)S(1)}, u32[]{:S(2)}, u32[]{:S(2)}) collective-permute-start(f32[3,1,32,64]{3,2,1,0:T(8,128)S(1)} %get-tuple-element.324), channel_id=1, source_target_pairs={{1,0},{2,1},{3,2},{4,3},{5,4},{6,5},{7,6},{9,8},{10,9},{11,10},{12... | collective-permute-start | bytes 73736 | tf_op jit(solution)/shard_map/while/body/eval_jaxpr/ppermute | solution.py:26
  39.4 4.3 %collective-permute-start.3 = (f32[3,1,32,64]{3,2,1,0:T(8,128)S(1)}, f32[3,1,32,64]{3,2,1,0:T(8,128)S(1)}, u32[]{:S(2)}, u32[]{:S(2)}) collective-permute-start(f32[3,1,32,64]{3,2,1,0:T(8,128)S(1)} %get-tuple-element.325), channel_id=1, source_target_pairs={{0,1},{1,2},{2,3},{3,4},{4,5},{5,6},{6,7},{8,9},{9,10},{10,11},{11... | collective-permute-start | bytes 73736 | tf_op jit(solution)/shard_map/while/body/eval_jaxpr/ppermute | solution.py:24
  44.0 6.2 %collective-permute-start.2 = (f32[3,1,32,64]{3,2,1,0:T(8,128)S(1)}, f32[3,1,32,64]{3,2,1,0:T(8,128)S(1)}, u32[]{:S(2)}, u32[]{:S(2)}) collective-permute-start(f32[3,1,32,64]{3,2,1,0:T(8,128)S(1)} %get-tuple-element.324), channel_id=1, source_target_pairs={{1,0},{2,1},{3,2},{4,3},{5,4},{6,5},{7,6},{9,8},{10,9},{11,10},{12... | collective-permute-start | bytes 73736 | tf_op jit(solution)/shard_map/while/body/eval_jaxpr/ppermute | solution.py:26
  47.1 4.3 %collective-permute-start.3 = (f32[3,1,32,64]{3,2,1,0:T(8,128)S(1)}, f32[3,1,32,64]{3,2,1,0:T(8,128)S(1)}, u32[]{:S(2)}, u32[]{:S(2)}) collective-permute-start(f32[3,1,32,64]{3,2,1,0:T(8,128)S(1)} %get-tuple-element.325), channel_id=1, source_target_pairs={{0,1},{1,2},{2,3},{3,4},{4,5},{5,6},{6,7},{8,9},{9,10},{10,11},{11... | collective-permute-start | bytes 73736 | tf_op jit(solution)/shard_map/while/body/eval_jaxpr/ppermute | solution.py:24
  52.6 6.8 %collective-permute-start = (f32[3,2,64,128]{3,2,1,0:T(8,128)S(1)}, f32[3,2,64,128]{3,2,1,0:T(8,128)S(1)}, u32[]{:S(2)}, u32[]{:S(2)}) collective-permute-start(f32[3,2,64,128]{3,2,1,0:T(8,128)S(1)} %get-tuple-element.307), channel_id=1, source_target_pairs={{0,1},{1,2},{2,3},{3,4},{4,5},{5,6},{6,7},{8,9},{9,10},{10,11},{11... | collective-permute-start | bytes 589832 | tf_op jit(solution)/shard_map/while/body/eval_jaxpr/ppermute | solution.py:24
  56.9 7.0 %collective-permute-start.1 = (f32[3,2,64,128]{3,2,1,0:T(8,128)S(1)}, f32[3,2,64,128]{3,2,1,0:T(8,128)S(1)}, u32[]{:S(2)}, u32[]{:S(2)}) collective-permute-start(f32[3,2,64,128]{3,2,1,0:T(8,128)S(1)} %get-tuple-element.311), channel_id=1, source_target_pairs={{1,0},{2,1},{3,2},{4,3},{5,4},{6,5},{7,6},{9,8},{10,9},{11,10},{12... | collective-permute-start | bytes 589832 | tf_op jit(solution)/shard_map/while/body/eval_jaxpr/ppermute | solution.py:26
  65.0 4.5 %collective-permute-start = (f32[3,2,64,128]{3,2,1,0:T(8,128)S(1)}, f32[3,2,64,128]{3,2,1,0:T(8,128)S(1)}, u32[]{:S(2)}, u32[]{:S(2)}) collective-permute-start(f32[3,2,64,128]{3,2,1,0:T(8,128)S(1)} %get-tuple-element.307), channel_id=1, source_target_pairs={{0,1},{1,2},{2,3},{3,4},{4,5},{5,6},{6,7},{8,9},{9,10},{10,11},{11... | collective-permute-start | bytes 589832 | tf_op jit(solution)/shard_map/while/body/eval_jaxpr/ppermute | solution.py:24
  66.9 7.0 %collective-permute-start.1 = (f32[3,2,64,128]{3,2,1,0:T(8,128)S(1)}, f32[3,2,64,128]{3,2,1,0:T(8,128)S(1)}, u32[]{:S(2)}, u32[]{:S(2)}) collective-permute-start(f32[3,2,64,128]{3,2,1,0:T(8,128)S(1)} %get-tuple-element.311), channel_id=1, source_target_pairs={{1,0},{2,1},{3,2},{4,3},{5,4},{6,5},{7,6},{9,8},{10,9},{11,10},{12... | collective-permute-start | bytes 589832 | tf_op jit(solution)/shard_map/while/body/eval_jaxpr/ppermute | solution.py:26
  75.0 4.5 %collective-permute-start = (f32[3,2,64,128]{3,2,1,0:T(8,128)S(1)}, f32[3,2,64,128]{3,2,1,0:T(8,128)S(1)}, u32[]{:S(2)}, u32[]{:S(2)}) collective-permute-start(f32[3,2,64,128]{3,2,1,0:T(8,128)S(1)} %get-tuple-element.307), channel_id=1, source_target_pairs={{0,1},{1,2},{2,3},{3,4},{4,5},{5,6},{6,7},{8,9},{9,10},{10,11},{11... | collective-permute-start | bytes 589832 | tf_op jit(solution)/shard_map/while/body/eval_jaxpr/ppermute | solution.py:24
  77.0 7.0 %collective-permute-start.1 = (f32[3,2,64,128]{3,2,1,0:T(8,128)S(1)}, f32[3,2,64,128]{3,2,1,0:T(8,128)S(1)}, u32[]{:S(2)}, u32[]{:S(2)}) collective-permute-start(f32[3,2,64,128]{3,2,1,0:T(8,128)S(1)} %get-tuple-element.311), channel_id=1, source_target_pairs={{1,0},{2,1},{3,2},{4,3},{5,4},{6,5},{7,6},{9,8},{10,9},{11,10},{12... | collective-permute-start | bytes 589832 | tf_op jit(solution)/shard_map/while/body/eval_jaxpr/ppermute | solution.py:26
  85.1 4.5 %collective-permute-start = (f32[3,2,64,128]{3,2,1,0:T(8,128)S(1)}, f32[3,2,64,128]{3,2,1,0:T(8,128)S(1)}, u32[]{:S(2)}, u32[]{:S(2)}) collective-permute-start(f32[3,2,64,128]{3,2,1,0:T(8,128)S(1)} %get-tuple-element.307), channel_id=1, source_target_pairs={{0,1},{1,2},{2,3},{3,4},{4,5},{5,6},{6,7},{8,9},{9,10},{10,11},{11... | collective-permute-start | bytes 589832 | tf_op jit(solution)/shard_map/while/body/eval_jaxpr/ppermute | solution.py:24
  87.0 7.0 %collective-permute-start.1 = (f32[3,2,64,128]{3,2,1,0:T(8,128)S(1)}, f32[3,2,64,128]{3,2,1,0:T(8,128)S(1)}, u32[]{:S(2)}, u32[]{:S(2)}) collective-permute-start(f32[3,2,64,128]{3,2,1,0:T(8,128)S(1)} %get-tuple-element.311), channel_id=1, source_target_pairs={{1,0},{2,1},{3,2},{4,3},{5,4},{6,5},{7,6},{9,8},{10,9},{11,10},{12... | collective-permute-start | bytes 589832 | tf_op jit(solution)/shard_map/while/body/eval_jaxpr/ppermute | solution.py:26
  95.1 4.5 %collective-permute-start = (f32[3,2,64,128]{3,2,1,0:T(8,128)S(1)}, f32[3,2,64,128]{3,2,1,0:T(8,128)S(1)}, u32[]{:S(2)}, u32[]{:S(2)}) collective-permute-start(f32[3,2,64,128]{3,2,1,0:T(8,128)S(1)} %get-tuple-element.307), channel_id=1, source_target_pairs={{0,1},{1,2},{2,3},{3,4},{4,5},{5,6},{6,7},{8,9},{9,10},{10,11},{11... | collective-permute-start | bytes 589832 | tf_op jit(solution)/shard_map/while/body/eval_jaxpr/ppermute | solution.py:24
  97.1 7.0 %collective-permute-start.1 = (f32[3,2,64,128]{3,2,1,0:T(8,128)S(1)}, f32[3,2,64,128]{3,2,1,0:T(8,128)S(1)}, u32[]{:S(2)}, u32[]{:S(2)}) collective-permute-start(f32[3,2,64,128]{3,2,1,0:T(8,128)S(1)} %get-tuple-element.311), channel_id=1, source_target_pairs={{1,0},{2,1},{3,2},{4,3},{5,4},{6,5},{7,6},{9,8},{10,9},{11,10},{12... | collective-permute-start | bytes 589832 | tf_op jit(solution)/shard_map/while/body/eval_jaxpr/ppermute | solution.py:26
  105.2 4.5 %collective-permute-start = (f32[3,2,64,128]{3,2,1,0:T(8,128)S(1)}, f32[3,2,64,128]{3,2,1,0:T(8,128)S(1)}, u32[]{:S(2)}, u32[]{:S(2)}) collective-permute-start(f32[3,2,64,128]{3,2,1,0:T(8,128)S(1)} %get-tuple-element.307), channel_id=1, source_target_pairs={{0,1},{1,2},{2,3},{3,4},{4,5},{5,6},{6,7},{8,9},{9,10},{10,11},{11... | collective-permute-start | bytes 589832 | tf_op jit(solution)/shard_map/while/body/eval_jaxpr/ppermute | solution.py:24
  107.1 7.0 %collective-permute-start.1 = (f32[3,2,64,128]{3,2,1,0:T(8,128)S(1)}, f32[3,2,64,128]{3,2,1,0:T(8,128)S(1)}, u32[]{:S(2)}, u32[]{:S(2)}) collective-permute-start(f32[3,2,64,128]{3,2,1,0:T(8,128)S(1)} %get-tuple-element.311), channel_id=1, source_target_pairs={{1,0},{2,1},{3,2},{4,3},{5,4},{6,5},{7,6},{9,8},{10,9},{11,10},{12... | collective-permute-start | bytes 589832 | tf_op jit(solution)/shard_map/while/body/eval_jaxpr/ppermute | solution.py:26
  115.2 4.5 %collective-permute-start = (f32[3,2,64,128]{3,2,1,0:T(8,128)S(1)}, f32[3,2,64,128]{3,2,1,0:T(8,128)S(1)}, u32[]{:S(2)}, u32[]{:S(2)}) collective-permute-start(f32[3,2,64,128]{3,2,1,0:T(8,128)S(1)} %get-tuple-element.307), channel_id=1, source_target_pairs={{0,1},{1,2},{2,3},{3,4},{4,5},{5,6},{6,7},{8,9},{9,10},{10,11},{11... | collective-permute-start | bytes 589832 | tf_op jit(solution)/shard_map/while/body/eval_jaxpr/ppermute | solution.py:24
  117.1 7.0 %collective-permute-start.1 = (f32[3,2,64,128]{3,2,1,0:T(8,128)S(1)}, f32[3,2,64,128]{3,2,1,0:T(8,128)S(1)}, u32[]{:S(2)}, u32[]{:S(2)}) collective-permute-start(f32[3,2,64,128]{3,2,1,0:T(8,128)S(1)} %get-tuple-element.311), channel_id=1, source_target_pairs={{1,0},{2,1},{3,2},{4,3},{5,4},{6,5},{7,6},{9,8},{10,9},{11,10},{12... | collective-permute-start | bytes 589832 | tf_op jit(solution)/shard_map/while/body/eval_jaxpr/ppermute | solution.py:26
  125.3 4.5 %collective-permute-start = (f32[3,2,64,128]{3,2,1,0:T(8,128)S(1)}, f32[3,2,64,128]{3,2,1,0:T(8,128)S(1)}, u32[]{:S(2)}, u32[]{:S(2)}) collective-permute-start(f32[3,2,64,128]{3,2,1,0:T(8,128)S(1)} %get-tuple-element.307), channel_id=1, source_target_pairs={{0,1},{1,2},{2,3},{3,4},{4,5},{5,6},{6,7},{8,9},{9,10},{10,11},{11... | collective-permute-start | bytes 589832 | tf_op jit(solution)/shard_map/while/body/eval_jaxpr/ppermute | solution.py:24
  127.2 7.0 %collective-permute-start.1 = (f32[3,2,64,128]{3,2,1,0:T(8,128)S(1)}, f32[3,2,64,128]{3,2,1,0:T(8,128)S(1)}, u32[]{:S(2)}, u32[]{:S(2)}) collective-permute-start(f32[3,2,64,128]{3,2,1,0:T(8,128)S(1)} %get-tuple-element.311), channel_id=1, source_target_pairs={{1,0},{2,1},{3,2},{4,3},{5,4},{6,5},{7,6},{9,8},{10,9},{11,10},{12... | collective-permute-start | bytes 589832 | tf_op jit(solution)/shard_map/while/body/eval_jaxpr/ppermute | solution.py:26
  135.3 11.9 %collective-permute-start.7 = (f32[3,4,64,128]{3,2,1,0:T(8,128)S(1)}, f32[3,4,64,128]{3,2,1,0:T(8,128)S(1)}, u32[]{:S(2)}, u32[]{:S(2)}) collective-permute-start(f32[3,4,64,128]{3,2,1,0:T(8,128)S(1)} %sub.66), channel_id=1, source_target_pairs={{0,8},{8,16},{16,24},{1,9},{9,17},{17,25},{2,10},{10,18},{18,26},{... | collective-permute-start | bytes 1179656 | tf_op jit(solution)/shard_map/ppermute | solution.py:36
  183.1 6.4 %collective-permute-start.6 = (f32[3,2,32,64]{3,2,1,0:T(8,128)S(1)}, f32[3,2,32,64]{3,2,1,0:T(8,128)S(1)}, u32[]{:S(2)}, u32[]{:S(2)}) collective-permute-start(f32[3,2,32,64]{3,2,1,0:T(8,128)S(1)} %get-tuple-element.390), channel_id=1, source_target_pairs={{0,8},{8,16},{16,24},{1,9},{9,17},{17,25},{2,10},{10,18},{18,26},{... | collective-permute-start | bytes 147464 | tf_op jit(solution)/shard_map/while/body/eval_jaxpr/ppermute | solution.py:36
  189.6 5.7 %collective-permute-start.4 = (f32[3,1,32,64]{3,2,1,0:T(8,128)S(1)}, f32[3,1,32,64]{3,2,1,0:T(8,128)S(1)}, u32[]{:S(2)}, u32[]{:S(2)}) collective-permute-start(f32[3,1,32,64]{3,2,1,0:T(8,128)S(1)} %get-tuple-element.340), channel_id=1, source_target_pairs={{1,0},{2,1},{3,2},{4,3},{5,4},{6,5},{7,6},{9,8},{10,9},{11,10},{12... | collective-permute-start | bytes 73736 | tf_op jit(solution)/shard_map/while/body/eval_jaxpr/while/body/eval_jaxpr/ppermute | solution.py:26
  192.2 4.3 %collective-permute-start.5 = (f32[3,1,32,64]{3,2,1,0:T(8,128)S(1)}, f32[3,1,32,64]{3,2,1,0:T(8,128)S(1)}, u32[]{:S(2)}, u32[]{:S(2)}) collective-permute-start(f32[3,1,32,64]{3,2,1,0:T(8,128)S(1)} %get-tuple-element.341), channel_id=1, source_target_pairs={{0,1},{1,2},{2,3},{3,4},{4,5},{5,6},{6,7},{8,9},{9,10},{10,11},{11... | collective-permute-start | bytes 73736 | tf_op jit(solution)/shard_map/while/body/eval_jaxpr/while/body/eval_jaxpr/ppermute | solution.py:24
  196.8 6.2 %collective-permute-start.4 = (f32[3,1,32,64]{3,2,1,0:T(8,128)S(1)}, f32[3,1,32,64]{3,2,1,0:T(8,128)S(1)}, u32[]{:S(2)}, u32[]{:S(2)}) collective-permute-start(f32[3,1,32,64]{3,2,1,0:T(8,128)S(1)} %get-tuple-element.340), channel_id=1, source_target_pairs={{1,0},{2,1},{3,2},{4,3},{5,4},{6,5},{7,6},{9,8},{10,9},{11,10},{12... | collective-permute-start | bytes 73736 | tf_op jit(solution)/shard_map/while/body/eval_jaxpr/while/body/eval_jaxpr/ppermute | solution.py:26
  199.9 4.3 %collective-permute-start.5 = (f32[3,1,32,64]{3,2,1,0:T(8,128)S(1)}, f32[3,1,32,64]{3,2,1,0:T(8,128)S(1)}, u32[]{:S(2)}, u32[]{:S(2)}) collective-permute-start(f32[3,1,32,64]{3,2,1,0:T(8,128)S(1)} %get-tuple-element.341), channel_id=1, source_target_pairs={{0,1},{1,2},{2,3},{3,4},{4,5},{5,6},{6,7},{8,9},{9,10},{10,11},{11... | collective-permute-start | bytes 73736 | tf_op jit(solution)/shard_map/while/body/eval_jaxpr/while/body/eval_jaxpr/ppermute | solution.py:24
  204.5 6.0 %collective-permute-start.6 = (f32[3,2,32,64]{3,2,1,0:T(8,128)S(1)}, f32[3,2,32,64]{3,2,1,0:T(8,128)S(1)}, u32[]{:S(2)}, u32[]{:S(2)}) collective-permute-start(f32[3,2,32,64]{3,2,1,0:T(8,128)S(1)} %get-tuple-element.390), channel_id=1, source_target_pairs={{0,8},{8,16},{16,24},{1,9},{9,17},{17,25},{2,10},{10,18},{18,26},{... | collective-permute-start | bytes 147464 | tf_op jit(solution)/shard_map/while/body/eval_jaxpr/ppermute | solution.py:36
  210.5 7.1 %collective-permute-start.4 = (f32[3,1,32,64]{3,2,1,0:T(8,128)S(1)}, f32[3,1,32,64]{3,2,1,0:T(8,128)S(1)}, u32[]{:S(2)}, u32[]{:S(2)}) collective-permute-start(f32[3,1,32,64]{3,2,1,0:T(8,128)S(1)} %get-tuple-element.340), channel_id=1, source_target_pairs={{1,0},{2,1},{3,2},{4,3},{5,4},{6,5},{7,6},{9,8},{10,9},{11,10},{12... | collective-permute-start | bytes 73736 | tf_op jit(solution)/shard_map/while/body/eval_jaxpr/while/body/eval_jaxpr/ppermute | solution.py:26
  214.4 4.3 %collective-permute-start.5 = (f32[3,1,32,64]{3,2,1,0:T(8,128)S(1)}, f32[3,1,32,64]{3,2,1,0:T(8,128)S(1)}, u32[]{:S(2)}, u32[]{:S(2)}) collective-permute-start(f32[3,1,32,64]{3,2,1,0:T(8,128)S(1)} %get-tuple-element.341), channel_id=1, source_target_pairs={{0,1},{1,2},{2,3},{3,4},{4,5},{5,6},{6,7},{8,9},{9,10},{10,11},{11... | collective-permute-start | bytes 73736 | tf_op jit(solution)/shard_map/while/body/eval_jaxpr/while/body/eval_jaxpr/ppermute | solution.py:24
  219.1 6.2 %collective-permute-start.4 = (f32[3,1,32,64]{3,2,1,0:T(8,128)S(1)}, f32[3,1,32,64]{3,2,1,0:T(8,128)S(1)}, u32[]{:S(2)}, u32[]{:S(2)}) collective-permute-start(f32[3,1,32,64]{3,2,1,0:T(8,128)S(1)} %get-tuple-element.340), channel_id=1, source_target_pairs={{1,0},{2,1},{3,2},{4,3},{5,4},{6,5},{7,6},{9,8},{10,9},{11,10},{12... | collective-permute-start | bytes 73736 | tf_op jit(solution)/shard_map/while/body/eval_jaxpr/while/body/eval_jaxpr/ppermute | solution.py:26
  222.1 4.3 %collective-permute-start.5 = (f32[3,1,32,64]{3,2,1,0:T(8,128)S(1)}, f32[3,1,32,64]{3,2,1,0:T(8,128)S(1)}, u32[]{:S(2)}, u32[]{:S(2)}) collective-permute-start(f32[3,1,32,64]{3,2,1,0:T(8,128)S(1)} %get-tuple-element.341), channel_id=1, source_target_pairs={{0,1},{1,2},{2,3},{3,4},{4,5},{5,6},{6,7},{8,9},{9,10},{10,11},{11... | collective-permute-start | bytes 73736 | tf_op jit(solution)/shard_map/while/body/eval_jaxpr/while/body/eval_jaxpr/ppermute | solution.py:24
  226.8 6.5 %collective-permute-start.6 = (f32[3,2,32,64]{3,2,1,0:T(8,128)S(1)}, f32[3,2,32,64]{3,2,1,0:T(8,128)S(1)}, u32[]{:S(2)}, u32[]{:S(2)}) collective-permute-start(f32[3,2,32,64]{3,2,1,0:T(8,128)S(1)} %get-tuple-element.390), channel_id=1, source_target_pairs={{0,8},{8,16},{16,24},{1,9},{9,17},{17,25},{2,10},{10,18},{18,26},{... | collective-permute-start | bytes 147464 | tf_op jit(solution)/shard_map/while/body/eval_jaxpr/ppermute | solution.py:36
  233.4 7.1 %collective-permute-start.4 = (f32[3,1,32,64]{3,2,1,0:T(8,128)S(1)}, f32[3,1,32,64]{3,2,1,0:T(8,128)S(1)}, u32[]{:S(2)}, u32[]{:S(2)}) collective-permute-start(f32[3,1,32,64]{3,2,1,0:T(8,128)S(1)} %get-tuple-element.340), channel_id=1, source_target_pairs={{1,0},{2,1},{3,2},{4,3},{5,4},{6,5},{7,6},{9,8},{10,9},{11,10},{12... | collective-permute-start | bytes 73736 | tf_op jit(solution)/shard_map/while/body/eval_jaxpr/while/body/eval_jaxpr/ppermute | solution.py:26
  237.3 4.3 %collective-permute-start.5 = (f32[3,1,32,64]{3,2,1,0:T(8,128)S(1)}, f32[3,1,32,64]{3,2,1,0:T(8,128)S(1)}, u32[]{:S(2)}, u32[]{:S(2)}) collective-permute-start(f32[3,1,32,64]{3,2,1,0:T(8,128)S(1)} %get-tuple-element.341), channel_id=1, source_target_pairs={{0,1},{1,2},{2,3},{3,4},{4,5},{5,6},{6,7},{8,9},{9,10},{10,11},{11... | collective-permute-start | bytes 73736 | tf_op jit(solution)/shard_map/while/body/eval_jaxpr/while/body/eval_jaxpr/ppermute | solution.py:24
  241.9 6.2 %collective-permute-start.4 = (f32[3,1,32,64]{3,2,1,0:T(8,128)S(1)}, f32[3,1,32,64]{3,2,1,0:T(8,128)S(1)}, u32[]{:S(2)}, u32[]{:S(2)}) collective-permute-start(f32[3,1,32,64]{3,2,1,0:T(8,128)S(1)} %get-tuple-element.340), channel_id=1, source_target_pairs={{1,0},{2,1},{3,2},{4,3},{5,4},{6,5},{7,6},{9,8},{10,9},{11,10},{12... | collective-permute-start | bytes 73736 | tf_op jit(solution)/shard_map/while/body/eval_jaxpr/while/body/eval_jaxpr/ppermute | solution.py:26
  245.0 4.3 %collective-permute-start.5 = (f32[3,1,32,64]{3,2,1,0:T(8,128)S(1)}, f32[3,1,32,64]{3,2,1,0:T(8,128)S(1)}, u32[]{:S(2)}, u32[]{:S(2)}) collective-permute-start(f32[3,1,32,64]{3,2,1,0:T(8,128)S(1)} %get-tuple-element.341), channel_id=1, source_target_pairs={{0,1},{1,2},{2,3},{3,4},{4,5},{5,6},{6,7},{8,9},{9,10},{10,11},{11... | collective-permute-start | bytes 73736 | tf_op jit(solution)/shard_map/while/body/eval_jaxpr/while/body/eval_jaxpr/ppermute | solution.py:24
where the time goes:
time: 256 us; the launch traced here: 252 us
  starting transfers between devices  91.7 us (36%)
  waiting for transfers between devices  69.9 us (27%)
  local copies, waits for them, and re-layouts  59.2 us (23%)
  other arithmetic  29.2 us (11%)
    ppermute x16, starting transfers between devices, padded_2(): lax.ppermute(head, axis, [((i + 1) % count, i) for i in range(ends)])  44 us
    ppermute x16, starting transfers between devices, padded_2(): lax.ppermute(tail, axis, [(i, (i + 1) % count) for i in range(ends)])  42.5 us
    ppermute x16, waiting for transfers between devices, padded_2(): lax.ppermute(head, axis, [((i + 1) % count, i) for i in range(ends)])  33.8 us
    another operation x1, local copies, waits for them, and re-layouts, restrict(): field.reshape(field.shape[0], field.shape[1] // 2, 2, field.shape[2] // 2...  27.3 us
    reshape x1, local copies, waits for them, and re-layouts, restrict(): field.reshape(field.shape[0], field.shape[1] // 2, 2, field.shape[2] // 2...  26.5 us
    ppermute x4, waiting for transfers between devices, passed_along(): return lax.ppermute(shard, axis, pairs)  25.3 us
    reduce_sum x2, other arithmetic, restrict(): return jnp.sum(blocks, axis=(2, 4, 6)) * 0.125  18.9 us
    ppermute x16, waiting for transfers between devices, padded_2(): lax.ppermute(tail, axis, [(i, (i + 1) % count) for i in range(ends)])  10.8 us
  transfers between devices with their start and end apart: 36, of which 28 were waited for; matrix products, arithmetic and copies ran while one was open for 1% of the time, Pallas kernels for 0%

commit v1 on v0

v1 whole, which is shorter than its diff:
```python
import functools

import jax
import jax.numpy as jnp
from jax import lax
from jax.experimental import pallas as pl
from jax.experimental.pallas import tpu as pltpu
from jax.sharding import PartitionSpec as P

FSTEPS = 16
CSTEPS = 2

fine_rate = 0.08
fine_advect = 0.04
coarse_rate = 0.16
coarse_advect = 0.16

PAD = 8
MESH = pl.DeviceIdType.MESH


def step(src, dst, layer, rows, rate, advect, shift):
    lanes = src.shape[-1]
    lane = lax.broadcasted_iota(jnp.int32, (8, lanes), 1)
    first, last = lane < shift, lane >= lanes - shift
    for row in range(rows[0], rows[1], 8):
        here = [src[layer, c, pl.ds(row, 8), :] for c in range(3)]
        ax, ay, az = (advect * v for v in here)
        xp, xm = rate - ax, rate + ax
        yp, ym = rate - ay, rate + ay
        zp = jnp.where(last, 0.0, rate - az)
        zm = jnp.where(first, 0.0, rate + az)
        for c in range(3):
            x_part = xp * src[layer + 1, c, pl.ds(row, 8), :] + xm * src[layer - 1, c, pl.ds(row, 8), :]
            y_part = yp * src[layer, c, pl.ds(row + 1, 8), :] + ym * src[layer, c, pl.ds(row - 1, 8), :]
            z_part = zp * pltpu.roll(here[c], lanes - shift, 1) + zm * pltpu.roll(here[c], shift, 1)
            dst[layer, c, pl.ds(row, 8), :] = (1.0 - 6.0 * rate) * here[c] + x_part + (y_part + z_part)


def kernel(S, N, x_ref, out_ref, state, level, ca, cb, old, adv, pk_old, pk_rch, pk_cs, rc_old, rc_rch, rc_cs,
           chg, rc_chg, spread, halo_send, halo_recv, small_send, small_recv, cs_send, cs_recv, chg_send, chg_recv):
    n, s = lax.axis_index("cuts"), lax.axis_index("space")
    W, NY, NZ = x_ref.shape[2], x_ref.shape[3], x_ref.shape[4]
    CW, CY = W // 2, NY // 2
    rounds = FSTEPS // W
    has_left, has_right = s > 0, s < S - 1
    before, after, following = lax.rem(s + S - 1, S), lax.rem(s + 1, S), lax.rem(n + 1, N)

    pairs = [(n, s - 1), (n, s + 1)]
    for d in (-1, 0, 1):
        pairs += [(n + 1, s + d), (n - 1, s + d)]
    conds = [(i >= 0) & (i < N) & (j >= 0) & (j < S) for i, j in pairs]
    if N > 2:
        for d in (-1, 0, 1):
            pairs += [(n + 2, s + d), (n - 2, s + d)]
            conds += [(n == 0) & (s + d >= 0) & (s + d < S), (n == 2) & (s + d >= 0) & (s + d < S)]
    barrier = pltpu.get_barrier_semaphore()
    count = 0
    for (i, j), cond in zip(pairs, conds):
        @pl.when(cond)
        def _():
            pl.semaphore_signal(barrier, inc=1, device_id=(i, j), device_id_type=MESH)
        count = count + jnp.where(cond, 1, 0)

    zero = jnp.zeros((PAD, NZ), jnp.float32)

    def clear(layer, _):
        for c in range(3):
            for top in (0, PAD + NY):
                for k in range(2):
                    state[k, layer, c, pl.ds(top, PAD), :] = zero
                for k in range(W - 1):
                    level[k, layer, c, pl.ds(top, PAD), :] = zero
        return 0

    def clear_halo(layer, _):
        for c in range(3):
            for row in range(PAD, PAD + NY, 8):
                for k in range(2):
                    state[k, layer, c, pl.ds(row, 8), :] = zero
                for k in range(W - 1):
                    level[k, layer, c, pl.ds(row, 8), :] = zero
        return 0

    lax.fori_loop(0, 3 * W, clear, 0)
    lax.fori_loop(jnp.where(has_left, W, 0), W, clear_halo, 0)
    lax.fori_loop(2 * W, jnp.where(has_right, 2 * W, 3 * W), clear_halo, 0)
    for i in range(3 * CW):
        for c in range(3):
            for row in range(0, CY + 2 * PAD, 8):
                if row < PAD or row >= PAD + CY:
                    ca[i, c, pl.ds(row, 8), :] = zero
                cb[i, c, pl.ds(row, 8), :] = zero
    for k in (0, 2):
        @pl.when(jnp.logical_not(has_left if k == 0 else has_right))
        def _():
            rc_cs[k] = jnp.zeros_like(rc_cs[k])
    for i in range(W):
        for c in range(3):
            state[0, W + i, c, pl.ds(PAD, NY), :] = x_ref[0, c, i]
    pl.semaphore_wait(barrier, count)

    inner = pl.ds(PAD, NY)

    def to_right(slot):
        return pltpu.make_async_remote_copy(
            src_ref=state.at[slot, pl.ds(W, W), :, inner], dst_ref=state.at[slot, pl.ds(0, W), :, inner],
            send_sem=halo_send.at[slot, 0], recv_sem=halo_recv.at[slot, 0], device_id=(n, after), device_id_type=MESH)

    def to_left(slot):
        return pltpu.make_async_remote_copy(
            src_ref=state.at[slot, pl.ds(W, W), :, inner], dst_ref=state.at[slot, pl.ds(2 * W, W), :, inner],
            send_sem=halo_send.at[slot, 1], recv_sem=halo_recv.at[slot, 1], device_id=(n, before), device_id_type=MESH)

    def send_halo(slot):
        @pl.when(has_right)
        def _():
            to_right(slot).start()

        @pl.when(has_left)
        def _():
            to_left(slot).start()

    def receive_halo(slot):
        @pl.when(has_left)
        def _():
            to_right(slot).wait_recv()

        @pl.when(has_right)
        def _():
            to_left(slot).wait_recv()

    def sent_halo(slot):
        @pl.when(has_right)
        def _():
            to_right(slot).wait_send()

        @pl.when(has_left)
        def _():
            to_left(slot).wait_send()

    even = lax.broadcasted_iota(jnp.int32, (CY, NZ), 1) % 2 == 0

    def restricted(read):
        total = (read(0, 0) + read(0, 1)) + (read(1, 0) + read(1, 1))
        other = jnp.where(even, pltpu.roll(total, NZ - 1, 1), pltpu.roll(total, 1, 1))
        return (total + other) * 0.125

    def packed(a, b):
        return jnp.where(even, a, b)

    def unpacked(v):
        return jnp.where(even, v, pltpu.roll(v, 1, 1)), jnp.where(even, pltpu.roll(v, NZ - 1, 1), v)

    def coarse_run(dest):
        lo = jnp.where(has_left, 1, CW)
        hi = jnp.where(has_right, 3 * CW - 1, 2 * CW)

        def one(i, _):
            step(ca, cb, i, (PAD, PAD + CY), coarse_rate, coarse_advect, 2)
            return 0

        def two(i, _):
            step(cb, dest, i, (PAD, PAD + CY), coarse_rate, coarse_advect, 2)
            return 0

        lax.fori_loop(lo, hi, one, 0)
        lax.fori_loop(CW, 2 * CW, two, 0)

    def small(k, src, dst, target):
        return pltpu.make_async_remote_copy(
            src_ref=src, dst_ref=dst, send_sem=small_send.at[k], recv_sem=small_recv.at[k],
            device_id=target, device_id_type=MESH)

    crow = pl.ds(PAD, CY)
    send_old = small(0, pk_old, rc_old, (following, s))
    send_rch = small(1, pk_rch, rc_rch, (following, s))

    send_halo(0)
    receive_halo(0)

    def restrict_layer(i, _):
        for c in range(3):
            ca[i, c, crow, :] = restricted(lambda l, r: state[0, 2 * i + l, c, pl.ds(PAD + r, CY, stride=2), :])
        return 0

    lax.fori_loop(0, 3 * CW, restrict_layer, 0)

    def one_round(r, _):
        slot = lax.rem(r, 2)
        for k in range(1, W + 1):
            src = state.at[slot] if k == 1 else level.at[k - 2]
            dst = state.at[1 - slot] if k == W else level.at[k - 1]
            lo = jnp.where(has_left, k, W)
            hi = jnp.where(has_right, 3 * W - k, 2 * W)

            def layer(i, _):
                step(src, dst, i, (PAD, PAD + NY), fine_rate, fine_advect, 1)
                return 0

            lax.fori_loop(lo, hi, layer, 0)
        sent_halo(slot)

        @pl.when(r < rounds - 1)
        def _():
            send_halo(1 - slot)

        @pl.when(r == 0)
        def _():
            coarse_run(old)

            @pl.when(n == 0)
            def _():
                for c in range(3):
                    pk_old[c] = packed(old[CW, c, crow, :], old[CW + 1, c, crow, :])
                send_old.start()

        @pl.when(r < rounds - 1)
        def _():
            receive_halo(1 - slot)
        return 0

    lax.fori_loop(0, rounds, one_round, 0)
    end = rounds % 2

    for i in range(CW):
        for c in range(3):
            base = old[CW + i, c, crow, :]
            for l in range(2):
                for r in range(2):
                    chg[2 * i + l, c, pl.ds(r, CY, stride=2), :] = (
                        state[end, W + 2 * i + l, c, pl.ds(PAD + r, CY, stride=2), :] - base)
    for c in range(3):
        rch = [restricted(lambda l, r: chg[2 * i + l, c, pl.ds(r, CY, stride=2), :]) for i in range(CW)]
        pk_rch[c] = packed(*rch)
        pk_cs[c] = packed(*(rch[i] + old[CW + i, c, crow, :] for i in range(CW)))

    def to_state(d, group):
        return pltpu.make_async_remote_copy(
            src_ref=pk_cs, dst_ref=rc_cs.at[1 - d], send_sem=cs_send.at[1 - d], recv_sem=cs_recv.at[1 - d],
            device_id=(group, lax.rem(s + d + S, S)), device_id_type=MESH)

    def each_target(do):
        for d in (0, 1, -1):
            @pl.when((s + d >= 0) & (s + d < S))
            def _():
                do(d)

    send_chg = pltpu.make_async_remote_copy(
        src_ref=chg.at[:, :, pl.ds(0, NY)], dst_ref=rc_chg, send_sem=chg_send, recv_sem=chg_recv, device_id=(following, s), device_id_type=MESH)

    if N > 2:
        @pl.when(n == 0)
        def _():
            each_target(lambda d: to_state(d, 2).start())

        @pl.when((n >= 1) & (n <= N - 3))
        def _():
            send_rch.start()

    @pl.when(n < N - 1)
    def _():
        send_chg.start()

    @pl.when(n == 1)
    def _():
        send_old.wait_recv()
        for c in range(3):
            for i, v in enumerate(unpacked(rc_old[c])):
                adv[CW + i, c, crow, :] = v

    if N > 2:
        @pl.when(n == 0)
        def _():
            each_target(lambda d: to_state(d, 2).wait_send())

        @pl.when((n >= 1) & (n <= N - 3))
        def _():
            send_rch.wait_send()

        @pl.when(n >= 2)
        def _():
            each_target(lambda d: to_state(-d, n).wait_recv())
            for k in range(3):
                for c in range(3):
                    for i, v in enumerate(unpacked(rc_cs[k, c])):
                        ca[k * CW + i, c, crow, :] = v
            coarse_run(adv)

            @pl.when(n <= N - 2)
            def _():
                send_rch.wait_recv()
                for c in range(3):
                    rch = unpacked(rc_rch[c])
                    pk_cs[c] = packed(*(adv[CW + i, c, crow, :] + rch[i] for i in range(CW)))
                each_target(lambda d: to_state(d, following).start())
                each_target(lambda d: to_state(d, following).wait_send())

    @pl.when(n == 0)
    def _():
        send_old.wait_send()
        out_ref[...] = x_ref[...]

    @pl.when(n > 0)
    def _():
        send_chg.wait_recv()
        for i in range(CW):
            for c in range(3):
                base = adv[CW + i, c, crow, :]
                for r in range(2):
                    spread[i, c, pl.ds(r, CY, stride=2), :] = base
        for i in range(W):
            for c in range(3):
                out_ref[0, c, i] = spread[i // 2, c, pl.ds(0, NY), :] + rc_chg[i, c]

    @pl.when(n < N - 1)
    def _():
        send_chg.wait_send()


def shards(S, N, starts):
    W, NY, NZ = starts.shape[2:]
    assert W == 4 and FSTEPS % W == 0 and CSTEPS == 2
    f32 = jnp.float32
    CW, CY = W // 2, NY // 2
    packed = pltpu.VMEM((3, CY, NZ), f32)
    coarse = pltpu.VMEM((3 * CW, 3, CY + 2 * PAD, NZ), f32)
    dma = pltpu.SemaphoreType.DMA
    return pl.pallas_call(
        functools.partial(kernel, S, N),
        out_shape=jax.ShapeDtypeStruct(starts.shape, f32),
        in_specs=[pl.BlockSpec(memory_space=pltpu.VMEM)],
        out_specs=pl.BlockSpec(memory_space=pltpu.VMEM),
        scratch_shapes=[
            pltpu.VMEM((2, 3 * W, 3, NY + 2 * PAD, NZ), f32),
            pltpu.VMEM((W - 1, 3 * W, 3, NY + 2 * PAD, NZ), f32),
            coarse, coarse, coarse, coarse,
            packed, packed, packed, packed, packed,
            pltpu.VMEM((3, 3, CY, NZ), f32),
            pltpu.VMEM((W, 3, NY + PAD, NZ), f32),
            pltpu.VMEM((W, 3, NY, NZ), f32),
            pltpu.VMEM((CW, 3, NY + PAD, NZ), f32),
            dma((2, 2)), dma((2, 2)), dma((2,)), dma((2,)), dma((3,)), dma((3,)), dma, dma,
        ],
        compiler_params=pltpu.CompilerParams(collective_id=0, has_side_effects=True),
    )(starts)


def solution(mesh):
    placed = P("cuts", None, "space", None, None)
    return jax.shard_map(
        functools.partial(shards, mesh.shape["space"], mesh.shape["cuts"]),
        mesh=mesh, in_specs=(placed,), out_specs=placed, check_vma=False)
```

time: 256 us -> 71.4 us (0.28); the launches traced: 252 us -> 71.2 us
  starting transfers between devices: 91.7 us -> 0 us
  waiting for transfers between devices: 69.9 us -> 0 us
  Pallas kernels: 0 us -> 69.4 us
  local copies, waits for them, and re-layouts: 59.2 us -> 1.77 us
  other arithmetic: 29.2 us -> 0 us
    ppermute x36 -> x0, starting transfers between devices: 91.7 us -> none  [the longest x16 44 us: padded_2(): lax.ppermute(head, axis, [((i + 1) % count, i) for i in range(ends)])]
    ppermute x36 -> x0, waiting for transfers between devices: 69.9 us -> none  [the longest x16 33.8 us: padded_2(): lax.ppermute(head, axis, [((i + 1) % count, i) for i in range(ends)])]
    pallas_call x0 -> x1, Pallas kernels: none -> 69.4 us  [shards(): pl.pallas_call(functools.partial(kernel, S, N), out_shape=jax.ShapeDtypeS...]
    another operation x1 -> x0, local copies, waits for them, and re-layouts: 27.3 us -> none  [restrict(): field.reshape(field.shape[0], field.shape[1] // 2, 2, field.shape[2] // 2...]
    reshape x4 -> x0, local copies, waits for them, and re-layouts: 27.1 us -> none  [the longest x1 26.5 us: restrict(): field.reshape(field.shape[0], field.shape[1] // 2, 2, field.shape[2] // 2...]
    reduce_sum x2 -> x0, other arithmetic: 18.9 us -> none  [restrict(): return jnp.sum(blocks, axis=(2, 4, 6)) * 0.125]
    select_n x11 -> x0, other arithmetic: 4.77 us -> none  [the longest x8 4.58 us: double_fine(): first = jnp.where(inside[None, :, None, None], first, 0.0)]
    sub x17 -> x0, other arithmetic: 4.25 us -> none  [the longest x16 4.21 us: advance(): return centre + rate * laplace - advect * convect]
  transfers between devices with their start and end apart: 36 -> 0, of which waited for: 28 -> 0; matrix products, arithmetic and copies ran while one was open for 1% -> 0% of each run, Pallas kernels for 0% -> 0%
where the time goes in v1:
time: 71.4 us; the launch traced here: 71.2 us
  Pallas kernels  69.4 us (97%)
  local copies, waits for them, and re-layouts  1.77 us (2%)
    pallas_call x1, Pallas kernels, shards(): pl.pallas_call(functools.partial(kernel, S, N), out_shape=jax.ShapeDtypeS...  69.4 us
    unnamed x1, local copies, waits for them, and re-layouts  1.77 us

profile of v1, /device:TPU:15, one launch (start us, length us, event | category | flops | bytes accessed | tf_op | source)
XLA Modules:
  0.0 71.2 jit_solution(477284802404506029)
XLA Ops:
  0.0 69.4 %shard_map.17 = f32[1,3,4,64,128]{4,3,2,1,0:T(8,128)} custom-call(f32[1,3,4,64,128]{4,3,2,1,0:T(8,128)} %x_ref.1), custom_call_target="tpu_custom_call" | custom-call | tf_op jit(solution)/shard_map/pallas_call | solution.py:329
  69.4 1.8 %copy.3 = f32[1,3,4,64,128]{4,3,2,1,0:T(8,128)} copy(f32[1,3,4,64,128]{4,3,2,1,0:T(8,128)} %shard_map.17) | data formatting | bytes 786432

commit v2 on v1

--- a/solution.py
+++ b/solution.py
@@ -19,22 +19,24 @@
 MESH = pl.DeviceIdType.MESH
 
 
-def step(src, dst, layer, rows, rate, advect, shift):
+def step(src, dst, layers, tiles, rate, advect, shift):
     lanes = src.shape[-1]
     lane = lax.broadcasted_iota(jnp.int32, (8, lanes), 1)
     first, last = lane < shift, lane >= lanes - shift
-    for row in range(rows[0], rows[1], 8):
-        here = [src[layer, c, pl.ds(row, 8), :] for c in range(3)]
-        ax, ay, az = (advect * v for v in here)
-        xp, xm = rate - ax, rate + ax
-        yp, ym = rate - ay, rate + ay
-        zp = jnp.where(last, 0.0, rate - az)
-        zm = jnp.where(first, 0.0, rate + az)
-        for c in range(3):
-            x_part = xp * src[layer + 1, c, pl.ds(row, 8), :] + xm * src[layer - 1, c, pl.ds(row, 8), :]
-            y_part = yp * src[layer, c, pl.ds(row + 1, 8), :] + ym * src[layer, c, pl.ds(row - 1, 8), :]
-            z_part = zp * pltpu.roll(here[c], lanes - shift, 1) + zm * pltpu.roll(here[c], shift, 1)
-            dst[layer, c, pl.ds(row, 8), :] = (1.0 - 6.0 * rate) * here[c] + x_part + (y_part + z_part)
+    for row in tiles:
+        for layer, keep in layers:
+            here = [src[layer, c, pl.ds(row, 8), :] for c in range(3)]
+            ax, ay, az = (advect * v for v in here)
+            xp, xm = rate - ax, rate + ax
+            yp, ym = rate - ay, rate + ay
+            zp = jnp.where(last, 0.0, rate - az)
+            zm = jnp.where(first, 0.0, rate + az)
+            for c in range(3):
+                x_part = xp * src[layer + 1, c, pl.ds(row, 8), :] + xm * src[layer - 1, c, pl.ds(row, 8), :]
+                y_part = yp * src[layer, c, pl.ds(row + 1, 8), :] + ym * src[layer, c, pl.ds(row - 1, 8), :]
+                z_part = zp * pltpu.roll(here[c], lanes - shift, 1) + zm * pltpu.roll(here[c], shift, 1)
+                new = (1.0 - 6.0 * rate) * here[c] + x_part + (y_part + z_part)
+                dst[layer, c, pl.ds(row, 8), :] = new if keep is None else jnp.where(keep, new, 0.0)
 
 
 def kernel(S, N, x_ref, out_ref, state, level, ca, cb, old, adv, pk_old, pk_rch, pk_cs, rc_old, rc_rch, rc_cs,
@@ -100,49 +102,60 @@
             state[0, W + i, c, pl.ds(PAD, NY), :] = x_ref[0, c, i]
     pl.semaphore_wait(barrier, count)
 
-    inner = pl.ds(PAD, NY)
-
-    def to_right(slot):
+    half = (NY // 8 + rounds) // 2 * 8
+    bounds = [half - 8 * r for r in range(rounds + 1)]
+    assert 8 <= bounds[-1] and bounds[0] < NY
+
+    def rows_of(r, piece):
+        return pl.ds(PAD, bounds[r]) if piece == 0 else pl.ds(PAD + bounds[r], NY - bounds[r])
+
+    def to_right(r, piece):
+        slot, rows = r % 2, rows_of(r, piece)
         return pltpu.make_async_remote_copy(
-            src_ref=state.at[slot, pl.ds(W, W), :, inner], dst_ref=state.at[slot, pl.ds(0, W), :, inner],
-            send_sem=halo_send.at[slot, 0], recv_sem=halo_recv.at[slot, 0], device_id=(n, after), device_id_type=MESH)
-
-    def to_left(slot):
+            src_ref=state.at[slot, pl.ds(W, W), :, rows], dst_ref=state.at[slot, pl.ds(0, W), :, rows],
+            send_sem=halo_send.at[slot, 0, piece], recv_sem=halo_recv.at[slot, 0, piece],
+            device_id=(n, after), device_id_type=MESH)
+
+    def to_left(r, piece):
+        slot, rows = r % 2, rows_of(r, piece)
         return pltpu.make_async_remote_copy(
-            src_ref=state.at[slot, pl.ds(W, W), :, inner], dst_ref=state.at[slot, pl.ds(2 * W, W), :, inner],
-            send_sem=halo_send.at[slot, 1], recv_sem=halo_recv.at[slot, 1], device_id=(n, before), device_id_type=MESH)
-
-    def send_halo(slot):
+            src_ref=state.at[slot, pl.ds(W, W), :, rows], dst_ref=state.at[slot, pl.ds(2 * W, W), :, rows],
+            send_sem=halo_send.at[slot, 1, piece], recv_sem=halo_recv.at[slot, 1, piece],
+            device_id=(n, before), device_id_type=MESH)
+
+    def send_halo(r, piece):
         @pl.when(has_right)
         def _():
-            to_right(slot).start()
+            to_right(r, piece).start()
 
         @pl.when(has_left)
         def _():
-            to_left(slot).start()
-
-    def receive_halo(slot):
+            to_left(r, piece).start()
+
+    def receive_halo(r, piece):
         @pl.when(has_left)
         def _():
-            to_right(slot).wait_recv()
+            to_right(r, piece).wait_recv()
 
         @pl.when(has_right)
         def _():
-            to_left(slot).wait_recv()
-
-    def sent_halo(slot):
-        @pl.when(has_right)
-        def _():
-            to_right(slot).wait_send()
-
-        @pl.when(has_left)
-        def _():
-            to_left(slot).wait_send()
+            to_left(r, piece).wait_recv()
+
+    def sent_halo(r):
+        for piece in range(2):
+            @pl.when(has_right)
+            def _():
+                to_right(r, piece).wait_send()
+
+            @pl.when(has_left)
+            def _():
+                to_left(r, piece).wait_send()
 
     even = lax.broadcasted_iota(jnp.int32, (CY, NZ), 1) % 2 == 0
 
     def restricted(read):
         total = (read(0, 0) + read(0, 1)) + (read(1, 0) + read(1, 1))
+        even = lax.broadcasted_iota(jnp.int32, total.shape, 1) % 2 == 0
         other = jnp.where(even, pltpu.roll(total, NZ - 1, 1), pltpu.roll(total, 1, 1))
         return (total + other) * 0.125
 
@@ -153,19 +166,12 @@
         return jnp.where(even, v, pltpu.roll(v, 1, 1)), jnp.where(even, pltpu.roll(v, NZ - 1, 1), v)
 
     def coarse_run(dest):
-        lo = jnp.where(has_left, 1, CW)
-        hi = jnp.where(has_right, 3 * CW - 1, 2 * CW)
-
-        def one(i, _):
-            step(ca, cb, i, (PAD, PAD + CY), coarse_rate, coarse_advect, 2)
-            return 0
-
-        def two(i, _):
-            step(cb, dest, i, (PAD, PAD + CY), coarse_rate, coarse_advect, 2)
-            return 0
-
-        lax.fori_loop(lo, hi, one, 0)
-        lax.fori_loop(CW, 2 * CW, two, 0)
+        tiles = range(PAD, PAD + CY, 8)
+        for i in range(1, CW + CW // 2):
+            keep = (has_left, has_right) if i < CW else (None, None)
+            step(ca, cb, ((i, keep[0]), (3 * CW - 1 - i, keep[1])), tiles, coarse_rate, coarse_advect, 2)
+        for i in range(CW, CW + CW // 2):
+            step(cb, dest, ((i, None), (3 * CW - 1 - i, None)), tiles, coarse_rate, coarse_advect, 2)
 
     def small(k, src, dst, target):
         return pltpu.make_async_remote_copy(
@@ -176,37 +182,47 @@
     send_old = small(0, pk_old, rc_old, (following, s))
     send_rch = small(1, pk_rch, rc_rch, (following, s))
 
-    send_halo(0)
-    receive_halo(0)
-
-    def restrict_layer(i, _):
-        for c in range(3):
-            ca[i, c, crow, :] = restricted(lambda l, r: state[0, 2 * i + l, c, pl.ds(PAD + r, CY, stride=2), :])
-        return 0
-
-    lax.fori_loop(0, 3 * CW, restrict_layer, 0)
-
-    def one_round(r, _):
-        slot = lax.rem(r, 2)
+    def fine_piece(r, piece):
+        bound = PAD + bounds[r]
         for k in range(1, W + 1):
-            src = state.at[slot] if k == 1 else level.at[k - 2]
-            dst = state.at[1 - slot] if k == W else level.at[k - 1]
-            lo = jnp.where(has_left, k, W)
-            hi = jnp.where(has_right, 3 * W - k, 2 * W)
-
-            def layer(i, _):
-                step(src, dst, i, (PAD, PAD + NY), fine_rate, fine_advect, 1)
+            src = state.at[r % 2] if k == 1 else level.at[k - 2]
+            dst = state.at[(r + 1) % 2] if k == W else level.at[k - 1]
+            if piece == 0:
+                tiles = list(range(PAD, bound - 8, 8)) + [bound - 8 - k]
+            else:
+                tiles = [bound - k] + list(range(bound, PAD + NY, 8))
+            if k == W and piece == 0 and r > 0:
+                sent_halo(r - 1)
+
+            def pair(i, _):
+                step(src, dst, ((i, has_left | (i >= W)), (3 * W - 1 - i, has_right | (i >= W))), tiles,
+                     fine_rate, fine_advect, 1)
                 return 0
 
-            lax.fori_loop(lo, hi, layer, 0)
-        sent_halo(slot)
-
-        @pl.when(r < rounds - 1)
-        def _():
-            send_halo(1 - slot)
-
-        @pl.when(r == 0)
-        def _():
+            lax.fori_loop(k, W + W // 2, pair, 0)
+
+    def restrict_piece(piece):
+        first, last = (0, bounds[0] // 2) if piece == 0 else (bounds[0] // 2, CY)
+
+        def restrict_layer(i, _):
+            for c in range(3):
+                ca[i, c, pl.ds(PAD + first, last - first), :] = restricted(
+                    lambda l, r: state[0, 2 * i + l, c, pl.ds(PAD + 2 * first + r, last - first, stride=2), :])
+            return 0
+
+        lax.fori_loop(0, 3 * CW, restrict_layer, 0)
+
+    for piece in range(2):
+        send_halo(0, piece)
+    for r in range(rounds):
+        for piece in range(2):
+            receive_halo(r, piece)
+            if r == 0:
+                restrict_piece(piece)
+            fine_piece(r, piece)
+            if r < rounds - 1:
+                send_halo(r + 1, piece)
+        if r == 0:
             coarse_run(old)
 
             @pl.when(n == 0)
@@ -214,13 +230,7 @@
                 for c in range(3):
                     pk_old[c] = packed(old[CW, c, crow, :], old[CW + 1, c, crow, :])
                 send_old.start()
-
-        @pl.when(r < rounds - 1)
-        def _():
-            receive_halo(1 - slot)
-        return 0
-
-    lax.fori_loop(0, rounds, one_round, 0)
+    sent_halo(rounds - 1)
     end = rounds % 2
 
     for i in range(CW):
@@ -340,7 +350,7 @@
             pltpu.VMEM((W, 3, NY + PAD, NZ), f32),
             pltpu.VMEM((W, 3, NY, NZ), f32),
             pltpu.VMEM((CW, 3, NY + PAD, NZ), f32),
-            dma((2, 2)), dma((2, 2)), dma((2,)), dma((2,)), dma((3,)), dma((3,)), dma, dma,
+            dma((2, 2, 2)), dma((2, 2, 2)), dma((2,)), dma((2,)), dma((3,)), dma((3,)), dma, dma,
         ],
         compiler_params=pltpu.CompilerParams(collective_id=0, has_side_effects=True),
     )(starts)

time: 71.4 us -> 83.7 us (1.17)
  Pallas kernels: 69.4 us -> 81.8 us
    pallas_call x1, Pallas kernels: 69.4 us -> 81.8 us  [shards(): pl.pallas_call(functools.partial(kernel, S, N), out_shape=jax.ShapeDtypeS...]
where the time goes in v2:
time: 83.7 us; the launch traced here: 83.6 us
  Pallas kernels  81.8 us (98%)
  local copies, waits for them, and re-layouts  1.77 us (2%)
    pallas_call x1, Pallas kernels, shards(): pl.pallas_call(functools.partial(kernel, S, N), out_shape=jax.ShapeDtypeS...  81.8 us
    unnamed x1, local copies, waits for them, and re-layouts  1.77 us

profile of v2, /device:TPU:15, one launch (start us, length us, event | category | flops | bytes accessed | tf_op | source)
XLA Modules:
  0.0 83.6 jit_solution(13918298171977618549)
XLA Ops:
  0.0 81.8 %shard_map.17 = f32[1,3,4,64,128]{4,3,2,1,0:T(8,128)} custom-call(f32[1,3,4,64,128]{4,3,2,1,0:T(8,128)} %x_ref.1), custom_call_target="tpu_custom_call" | custom-call | tf_op jit(solution)/shard_map/pallas_call | solution.py:339
  81.8 1.8 %copy.3 = f32[1,3,4,64,128]{4,3,2,1,0:T(8,128)} copy(f32[1,3,4,64,128]{4,3,2,1,0:T(8,128)} %shard_map.17) | data formatting | bytes 786432

commit v3 on v1

--- a/solution.py
+++ b/solution.py
@@ -19,22 +19,39 @@
 MESH = pl.DeviceIdType.MESH
 
 
-def step(src, dst, layer, rows, rate, advect, shift):
+GROUP = 8
+
+
+def step(src, dst, layers, rows, rate, advect, shift):
     lanes = src.shape[-1]
     lane = lax.broadcasted_iota(jnp.int32, (8, lanes), 1)
     first, last = lane < shift, lane >= lanes - shift
-    for row in range(rows[0], rows[1], 8):
-        here = [src[layer, c, pl.ds(row, 8), :] for c in range(3)]
-        ax, ay, az = (advect * v for v in here)
-        xp, xm = rate - ax, rate + ax
-        yp, ym = rate - ay, rate + ay
-        zp = jnp.where(last, 0.0, rate - az)
-        zm = jnp.where(first, 0.0, rate + az)
-        for c in range(3):
-            x_part = xp * src[layer + 1, c, pl.ds(row, 8), :] + xm * src[layer - 1, c, pl.ds(row, 8), :]
-            y_part = yp * src[layer, c, pl.ds(row + 1, 8), :] + ym * src[layer, c, pl.ds(row - 1, 8), :]
-            z_part = zp * pltpu.roll(here[c], lanes - shift, 1) + zm * pltpu.roll(here[c], shift, 1)
-            dst[layer, c, pl.ds(row, 8), :] = (1.0 - 6.0 * rate) * here[c] + x_part + (y_part + z_part)
+    items = [(layer, keep, row) for row in range(rows[0], rows[1], 8) for layer, keep in layers]
+    groups = [items[i:i + GROUP] for i in range(0, len(items), GROUP)]
+
+    def shifted(group):
+        here = [[src[layer, c, pl.ds(row, 8), :] for c in range(3)] for layer, keep, row in group]
+        return [[(v, pltpu.roll(v, lanes - shift, 1), pltpu.roll(v, shift, 1)) for v in vs] for vs in here]
+
+    ready = shifted(groups[0])
+    for g, group in enumerate(groups):
+        values, ready = ready, shifted(groups[g + 1]) if g + 1 < len(groups) else None
+        new = []
+        for (layer, keep, row), vs in zip(group, values):
+            ax, ay, az = (advect * v[0] for v in vs)
+            xp, xm = rate - ax, rate + ax
+            yp, ym = rate - ay, rate + ay
+            zp = jnp.where(last, 0.0, rate - az)
+            zm = jnp.where(first, 0.0, rate + az)
+            for c in range(3):
+                x_part = xp * src[layer + 1, c, pl.ds(row, 8), :] + xm * src[layer - 1, c, pl.ds(row, 8), :]
+                y_part = yp * src[layer, c, pl.ds(row + 1, 8), :] + ym * src[layer, c, pl.ds(row - 1, 8), :]
+                z_part = zp * vs[c][1] + zm * vs[c][2]
+                value = ((1.0 - 6.0 * rate) * vs[c][0] + x_part) + (y_part + z_part)
+                new.append(value if keep is None else jnp.where(keep, value, 0.0))
+        for j, (layer, keep, row) in enumerate(group):
+            for c in range(3):
+                dst[layer, c, pl.ds(row, 8), :] = new[3 * j + c]
 
 
 def kernel(S, N, x_ref, out_ref, state, level, ca, cb, old, adv, pk_old, pk_rch, pk_cs, rc_old, rc_rch, rc_cs,
@@ -153,19 +170,12 @@
         return jnp.where(even, v, pltpu.roll(v, 1, 1)), jnp.where(even, pltpu.roll(v, NZ - 1, 1), v)
 
     def coarse_run(dest):
-        lo = jnp.where(has_left, 1, CW)
-        hi = jnp.where(has_right, 3 * CW - 1, 2 * CW)
-
-        def one(i, _):
-            step(ca, cb, i, (PAD, PAD + CY), coarse_rate, coarse_advect, 2)
-            return 0
-
-        def two(i, _):
-            step(cb, dest, i, (PAD, PAD + CY), coarse_rate, coarse_advect, 2)
-            return 0
-
-        lax.fori_loop(lo, hi, one, 0)
-        lax.fori_loop(CW, 2 * CW, two, 0)
+        rows = (PAD, PAD + CY)
+        for i in range(1, CW + CW // 2):
+            keep = (has_left, has_right) if i < CW else (None, None)
+            step(ca, cb, ((i, keep[0]), (3 * CW - 1 - i, keep[1])), rows, coarse_rate, coarse_advect, 2)
+        for i in range(CW, CW + CW // 2):
+            step(cb, dest, ((i, None), (3 * CW - 1 - i, None)), rows, coarse_rate, coarse_advect, 2)
 
     def small(k, src, dst, target):
         return pltpu.make_async_remote_copy(
@@ -191,14 +201,13 @@
         for k in range(1, W + 1):
             src = state.at[slot] if k == 1 else level.at[k - 2]
             dst = state.at[1 - slot] if k == W else level.at[k - 1]
-            lo = jnp.where(has_left, k, W)
-            hi = jnp.where(has_right, 3 * W - k, 2 * W)
-
-            def layer(i, _):
-                step(src, dst, i, (PAD, PAD + NY), fine_rate, fine_advect, 1)
+
+            def pair(i, _):
+                step(src, dst, ((i, has_left | (i >= W)), (3 * W - 1 - i, has_right | (i >= W))),
+                     (PAD, PAD + NY), fine_rate, fine_advect, 1)
                 return 0
 
-            lax.fori_loop(lo, hi, layer, 0)
+            lax.fori_loop(k, W + W // 2, pair, 0)
         sent_halo(slot)
 
         @pl.when(r < rounds - 1)

time: 71.4 us -> 61.7 us (0.86)
  Pallas kernels: 69.4 us -> 59.8 us
    pallas_call x1, Pallas kernels: 69.4 us -> 59.8 us  [shards(): pl.pallas_call(functools.partial(kernel, S, N), out_shape=jax.ShapeDtypeS...]
where the time goes in v3:
time: 61.7 us; the launch traced here: 61.5 us
  Pallas kernels  59.8 us (97%)
  local copies, waits for them, and re-layouts  1.77 us (3%)
    pallas_call x1, Pallas kernels, shards(): pl.pallas_call(functools.partial(kernel, S, N), out_shape=jax.ShapeDtypeS...  59.8 us
    unnamed x1, local copies, waits for them, and re-layouts  1.77 us

profile of v3, /device:TPU:15, one launch (start us, length us, event | category | flops | bytes accessed | tf_op | source)
XLA Modules:
  0.0 61.5 jit_solution(10543264390553849341)
XLA Ops:
  0.0 59.8 %shard_map.17 = f32[1,3,4,64,128]{4,3,2,1,0:T(8,128)} custom-call(f32[1,3,4,64,128]{4,3,2,1,0:T(8,128)} %x_ref.1), custom_call_target="tpu_custom_call" | custom-call | tf_op jit(solution)/shard_map/pallas_call | solution.py:338
  59.8 1.8 %copy.3 = f32[1,3,4,64,128]{4,3,2,1,0:T(8,128)} copy(f32[1,3,4,64,128]{4,3,2,1,0:T(8,128)} %shard_map.17) | data formatting | bytes 786432
